TPU v7x, 128 devices: a whole 4x4x4 slice. The times are simulated.
128 devices in a mesh: prob: 1, feat: 128 (over z, y, x, core).
Axes of the slice: x: 4, y: 4, z: 4, core: 2. Of those that a mesh axis runs over, the one named last changes fastest.
Arguments:
- design: bfloat16 [16384, 32768], P('prob', 'feat')
- coef_init: float32 [32768, 3], P(('prob', 'feat'))
- targets: float32 [16384, 3], P('prob')
- step_sizes: float32 [32768], P(('prob', 'feat'))
Outputs:
- output 1: float32 [32768, 3], P(('prob', 'feat'))
- output 2: float32 [16384, 3], P('prob')
All inputs are finite; a program needn't handle non-finite values.
Results may differ from a plain program's by a relative error of at most 0.00440094.
Values are sent between devices in bfloat16 or wider.
A program may use at most 1 GiB of HBM per device.

v0:
```python
import jax
import jax.numpy as jnp
from jax import lax
from jax.sharding import PartitionSpec as P

SWEEPS = 6
COMBINE_WEIGHT = 0.8


def solution(mesh):
    group_size = mesh.shape['feat']

    def local_run(x_local, coef_local, targets_local, step_local):
        samples = x_local.shape[0]
        features = x_local.shape[1] * group_size
        lasso_weight = 0.3 * group_size / features ** 0.5
        step_col = step_local[:, None]
        thresholds = step_col * lasso_weight

        def summed_product(values):
            product = jnp.dot(x_local, values.astype(jnp.bfloat16), preferred_element_type=jnp.float32)
            return lax.psum(product.astype(jnp.bfloat16).astype(jnp.float32), 'feat')

        weights = coef_local
        residual = targets_local - summed_product(weights)
        for _ in range(SWEEPS):
            gradient = lax.dot_general(x_local, residual.astype(jnp.bfloat16), (((0,), (0,)), ((), ())), preferred_element_type=jnp.float32) / samples
            stepped = weights + step_col * gradient
            shrunk = jnp.sign(stepped) * jnp.maximum(jnp.abs(stepped) - thresholds, 0.0)
            change = shrunk - weights
            weights = weights + COMBINE_WEIGHT * change
            residual = residual - COMBINE_WEIGHT * summed_product(change)
        return weights, residual

    return jax.shard_map(local_run, mesh=mesh, in_specs=(P('prob', 'feat'), P(('prob', 'feat'), None), P('prob', None), P(('prob', 'feat'))), out_specs=(P(('prob', 'feat'), None), P('prob', None)), check_vma=False)
```

profile of v0, /device:TPU:1, one launch (start us, length us, event | category | flops | bytes accessed | tf_op | source)
XLA Modules:
  0.0 1110.9 jit_solution(12028436447261084910)
XLA Ops:
  7.2 0.0 all-reduce.8.cloned.1.call-start
  7.2 6.4 fusion
  13.6 0.0 all-reduce.8.cloned.1.call-update
  13.7 0.0 all-reduce.10.cloned.1.call-start
  13.7 149.9 %all-reduce.8.cloned.1.call-done = f32[16384,3]{0,1:T(4,128)} async-done(((f32[16384,3]{0,1:T(4,128)}), f32[16384,3]{0,1:T(4,128)}) %all-reduce.8.cloned.1.call-update) | async-done | bytes 196624 | tf_op jit(solution)/shard_map/psum | solution.py:22
  163.6 1.2 sub.77
  164.8 4.8 multiply_subtract_fusion.14
  169.6 3.0 fusion.2
  172.6 0.0 all-reduce.12.cloned.1.call-start
  172.7 145.2 %all-reduce.10.cloned.1.call-done = f32[16384,3]{0,1:T(4,128)} async-done(((f32[16384,3]{0,1:T(4,128)}), f32[16384,3]{0,1:T(4,128)}) %all-reduce.10.cloned.1.call-update) | async-done | bytes 196624 | tf_op jit(solution)/shard_map/psum | solution.py:22
  317.9 4.7 multiply_add_fusion.4
  322.6 6.4 fusion.4
  329.0 0.0 all-reduce.14.cloned.1.call-start
  329.1 145.2 %all-reduce.12.cloned.1.call-done = f32[16384,3]{0,1:T(4,128)} async-done(((f32[16384,3]{0,1:T(4,128)}), f32[16384,3]{0,1:T(4,128)}) %all-reduce.12.cloned.1.call-update) | async-done | bytes 196624 | tf_op jit(solution)/shard_map/psum | solution.py:22
  474.3 1.1 multiply_subtract_fusion.4
  475.4 4.6 multiply_subtract_fusion.12
  480.0 6.4 fusion.6
  486.4 0.0 all-reduce.16.cloned.1.call-start
  486.4 145.2 %all-reduce.14.cloned.1.call-done = f32[16384,3]{0,1:T(4,128)} async-done(((f32[16384,3]{0,1:T(4,128)}), f32[16384,3]{0,1:T(4,128)}) %all-reduce.14.cloned.1.call-update) | async-done | bytes 196624 | tf_op jit(solution)/shard_map/psum | solution.py:22
  631.6 4.7 multiply_add_fusion.2
  636.4 6.4 fusion.8
  642.7 0.0 all-reduce.18.cloned.1.call-start
  642.8 145.2 %all-reduce.16.cloned.1.call-done = f32[16384,3]{0,1:T(4,128)} async-done(((f32[16384,3]{0,1:T(4,128)}), f32[16384,3]{0,1:T(4,128)}) %all-reduce.16.cloned.1.call-update) | async-done | bytes 196624 | tf_op jit(solution)/shard_map/psum | solution.py:22
  788.0 1.1 multiply_subtract_fusion.2
  789.1 4.6 multiply_subtract_fusion.10
  793.7 6.4 fusion.10
  800.1 0.0 all-reduce.20.cloned.1.call-start
  800.1 145.2 %all-reduce.18.cloned.1.call-done = f32[16384,3]{0,1:T(4,128)} async-done(((f32[16384,3]{0,1:T(4,128)}), f32[16384,3]{0,1:T(4,128)}) %all-reduce.18.cloned.1.call-update) | async-done | bytes 196624 | tf_op jit(solution)/shard_map/psum | solution.py:22
  945.3 5.3 multiply_add_fusion
  950.7 6.4 fusion.12
  957.0 145.3 %all-reduce.20.cloned.1.call-done = f32[16384,3]{0,1:T(4,128)} async-done(((f32[16384,3]{0,1:T(4,128)}), f32[16384,3]{0,1:T(4,128)}) %all-reduce.20.cloned.1.call-update) | async-done | bytes 196624 | tf_op jit(solution)/shard_map/psum | solution.py:22
  1102.3 1.8 multiply_subtract_fusion
  (21 shorter events, 0.1 us)
Async XLA Ops:
  7.2 157.6 %copy-start.5 = (f32[256,3]{0,1:T(4,128)S(1)}, f32[256,3]{0,1:T(4,128)}, u32[]{:S(2)}) copy-start(f32[256,3]{0,1:T(4,128)} %param.5) | copy-start | bytes 9220
  7.2 6.5 copy-start.6
  7.2 156.4 %copy-start.4 = (f32[16384,3]{0,1:T(4,128)S(1)}, f32[16384,3]{0,1:T(4,128)}, u32[]{:S(2)}) copy-start(f32[16384,3]{0,1:T(4,128)} %param.6) | copy-start | bytes 589828
  7.2 156.4 %all-reduce.8.cloned.1.call-start = ((), (), s32[]{:S(2)}) async-start(), calls=%async_computation | async-start | bytes 524288 | tf_op jit(solution)/shard_map/psum | solution.py:22
  13.7 304.3 %all-reduce.10.cloned.1.call-start = ((), (), s32[]{:S(2)}) async-start(), calls=%async_computation.1 | async-start | bytes 524288 | tf_op jit(solution)/shard_map/psum | solution.py:22
  163.6 6.0 copy-start
  172.6 301.6 %all-reduce.12.cloned.1.call-start = ((), (), s32[]{:S(2)}) async-start(), calls=%async_computation.2 | async-start | bytes 524288 | tf_op jit(solution)/shard_map/psum | solution.py:22
  317.9 156.4 %copy-start.3 = (f32[16384,3]{0,1:T(4,128)S(1)}, f32[16384,3]{0,1:T(4,128)}, u32[]{:S(2)}) copy-start(f32[16384,3]{0,1:T(4,128)} %all-reduce.10.cloned.1.call-done) | copy-start | bytes 589828
  329.0 302.6 %all-reduce.14.cloned.1.call-start = ((), (), s32[]{:S(2)}) async-start(), calls=%async_computation.3 | async-start | bytes 524288 | tf_op jit(solution)/shard_map/psum | solution.py:22
  486.4 301.6 %all-reduce.16.cloned.1.call-start = ((), (), s32[]{:S(2)}) async-start(), calls=%async_computation.4 | async-start | bytes 524288 | tf_op jit(solution)/shard_map/psum | solution.py:22
  631.6 156.4 %copy-start.1 = (f32[16384,3]{0,1:T(4,128)S(1)}, f32[16384,3]{0,1:T(4,128)}, u32[]{:S(2)}) copy-start(f32[16384,3]{0,1:T(4,128)} %all-reduce.14.cloned.1.call-done) | copy-start | bytes 589828
  642.7 302.6 %all-reduce.18.cloned.1.call-start = ((), (), s32[]{:S(2)}) async-start(), calls=%async_computation.5 | async-start | bytes 524288 | tf_op jit(solution)/shard_map/psum | solution.py:22
  800.1 302.2 %all-reduce.20.cloned.1.call-start = ((), (), s32[]{:S(2)}) async-start(), calls=%async_computation.6 | async-start | bytes 524288 | tf_op jit(solution)/shard_map/psum | solution.py:22
  945.3 157.0 %copy-start.2 = (f32[16384,3]{0,1:T(4,128)S(1)}, f32[16384,3]{0,1:T(4,128)}, u32[]{:S(2)}) copy-start(f32[16384,3]{0,1:T(4,128)} %all-reduce.18.cloned.1.call-done) | copy-start | bytes 589828
Sparse Core Ops, SparseCore 0:
  13.8 149.7 all-reduce.7
  172.8 145.1 all-reduce.9
  329.1 145.1 all-reduce.11
  486.5 145.1 all-reduce.13
  642.9 145.1 all-reduce.15
  800.2 145.1 all-reduce.17
  957.2 145.1 all-reduce.19
where the time goes:
time: 1110 us
  waiting for transfers between devices  1020 us (92%)
  matrix products  69.9 us (6%)
  between operations  14.2 us (1%)
    psum x7, waiting for transfers between devices, summed_product(): return lax.psum(product.astype(jnp.bfloat16).astype(jnp.float32), 'feat')  1020 us
    dot_general x7, matrix products, summed_product(): jnp.dot(x_local, values.astype(jnp.bfloat16), preferred_element_type=jnp....  41.1 us
    dot_general x6, matrix products, local_run(): lax.dot_general(x_local, residual.astype(jnp.bfloat16), (((0,), (0,)), ((...  28.7 us
  transfers between devices with their start and end apart: 7, of which 7 were waited for; matrix products, arithmetic and copies ran while one was open for 0% of the time, Pallas kernels for 0%

commit v1 on v0

v1 whole, which is shorter than its diff:
```python
import jax
import jax.numpy as jnp
from jax import lax
from jax.experimental import pallas as pl
from jax.experimental.pallas import tpu as pltpu
from jax.sharding import PartitionSpec as P

SWEEPS = 6
COMBINE_WEIGHT = 0.8
ROWS = 4
PIECE = 128


def solution(mesh):
    group = mesh.shape['feat']

    def body(x_hbm, w_in, y_hbm, eta_in, w_out, r_out,
             x_v, w_s, dw_s, u_send, u_recv, r_send, r_all, r_own, g_s,
             x_sem, y_sem, us_sem, ur_sem, rs_sem, rr_sem, fs_sem, fr_sem):
        me = lax.axis_index('feat')
        samples = x_hbm.shape[0]
        blk = x_hbm.shape[1]
        features = blk * group
        lasso_weight = 0.3 * group / features ** 0.5
        n_tiles = samples // 256
        tiles_per_load = n_tiles // x_sem.shape[0]
        load_rows = tiles_per_load * 256

        def x_load(i):
            rows = pl.ds(i * load_rows, load_rows)
            return pltpu.make_async_copy(x_hbm.at[rows], x_v.at[rows], x_sem.at[i])

        for i in range(x_sem.shape[0]):
            x_load(i).start()
        y_load = pltpu.make_async_copy(y_hbm.at[:, pl.ds(pl.multiple_of(me * PIECE, PIECE), PIECE)], r_own.at[pl.ds(0, 3)], y_sem)
        r_own[...] = jnp.zeros_like(r_own)

        barrier = pltpu.get_barrier_semaphore()

        def greet(i, carry):
            pl.semaphore_signal(barrier, inc=1, device_id={'feat': lax.rem(me + i, group)}, device_id_type=pl.DeviceIdType.MESH)
            return carry

        lax.fori_loop(1, group, greet, 0)

        w_s[...] = jnp.zeros_like(w_s)
        w_s[pl.ds(0, 3), :] = w_in[...]
        dw_s[...] = w_s[...].astype(jnp.bfloat16)
        step = eta_in[...]
        thr = step * lasso_weight

        def u_tile(c):
            xt = x_v[pl.ds(pl.multiple_of(c * 256, 256), 256), :]
            u = lax.dot_general(dw_s[...], xt, (((1,), (1,)), ((), ())), preferred_element_type=jnp.float32)
            ub = u.astype(jnp.bfloat16)
            u_send[2 * c] = ub[:ROWS, :PIECE]
            u_send[2 * c + 1] = ub[:ROWS, PIECE:]

        def u_copy(dest):
            return pltpu.make_async_remote_copy(
                src_ref=u_send.at[dest], dst_ref=u_recv.at[me], send_sem=us_sem, recv_sem=ur_sem,
                device_id={'feat': dest}, device_id_type=pl.DeviceIdType.MESH)

        def u_all():
            return pltpu.make_async_remote_copy(
                src_ref=u_send.at[pl.ds(0, group - 1)], dst_ref=u_recv.at[pl.ds(0, group - 1)], send_sem=us_sem, recv_sem=ur_sem,
                device_id={'feat': me}, device_id_type=pl.DeviceIdType.MESH)

        def r_copy(dest):
            return pltpu.make_async_remote_copy(
                src_ref=r_send, dst_ref=r_all.at[me], send_sem=rs_sem, recv_sem=rr_sem,
                device_id={'feat': dest}, device_id_type=pl.DeviceIdType.MESH)

        def r_gather():
            return pltpu.make_async_remote_copy(
                src_ref=r_all.at[pl.ds(0, group - 1)], dst_ref=r_all.at[pl.ds(0, group - 1)], send_sem=rs_sem, recv_sem=rr_sem,
                device_id={'feat': me}, device_id_type=pl.DeviceIdType.MESH)

        def send(copy):
            def one(i, carry):
                copy(lax.rem(me + i, group)).start()
                return carry
            lax.fori_loop(1, group, one, 0)

        def scatter_and_sum():
            send(u_copy)
            u_recv[me] = u_send[me]
            u_all().wait_recv()
            u_all().wait_send()
            acc = jnp.zeros((ROWS, PIECE), jnp.float32)
            for s in range(0, group, 16):
                acc = acc + jnp.sum(u_recv[pl.ds(s, 16)].astype(jnp.float32), axis=0)
            return acc

        y_load.start()
        for i in range(x_sem.shape[0]):
            x_load(i).wait()
            def tiles(c, carry, i=i):
                u_tile(i * tiles_per_load + c)
                return carry
            lax.fori_loop(0, tiles_per_load, tiles, 0, unroll=True)
        pl.semaphore_wait(barrier, group - 1)
        y_load.wait()
        r_own[...] = r_own[...] - scatter_and_sum()

        def sweep(t, carry):
            rb = r_own[...].astype(jnp.bfloat16)
            r_send[...] = rb
            r_all[me] = rb
            send(r_copy)
            r_gather().wait_recv()
            r_gather().wait_send()
            g = jnp.zeros((ROWS, blk), jnp.float32)
            for c in range(n_tiles):
                lhs = jnp.concatenate([r_all[2 * c], r_all[2 * c + 1]], axis=1)
                g = g + jnp.dot(lhs, x_v[pl.ds(c * 256, 256), :], preferred_element_type=jnp.float32)
            w = w_s[pl.ds(0, ROWS), :]
            v = w + step * (g / samples)
            v = jnp.maximum(v - thr, 0.0) + jnp.minimum(v + thr, 0.0)
            dw = v - w
            w_s[pl.ds(0, ROWS), :] = w + COMBINE_WEIGHT * dw
            dw_s[pl.ds(0, ROWS), :] = dw.astype(jnp.bfloat16)

            def tiles(c, carry):
                u_tile(c)
                return carry
            lax.fori_loop(0, n_tiles, tiles, 0, unroll=8)
            r_own[...] = r_own[...] - COMBINE_WEIGHT * scatter_and_sum()
            return carry

        lax.fori_loop(0, SWEEPS, sweep, 0)
        w_out[...] = w_s[pl.ds(0, 3), :]

        mine = pl.ds(pl.multiple_of(me * PIECE, PIECE), PIECE)
        r_out[:, mine] = r_own[...]

        def f_copy(dest):
            return pltpu.make_async_remote_copy(
                src_ref=r_own, dst_ref=r_out.at[:, mine], send_sem=fs_sem, recv_sem=fr_sem,
                device_id={'feat': dest}, device_id_type=pl.DeviceIdType.MESH)
        send(f_copy)
        done = pltpu.make_async_remote_copy(
            src_ref=r_out.at[:, pl.ds(0, (group - 1) * PIECE)], dst_ref=r_out.at[:, pl.ds(0, (group - 1) * PIECE)], send_sem=fs_sem, recv_sem=fr_sem,
            device_id={'feat': me}, device_id_type=pl.DeviceIdType.MESH)
        done.wait_recv()
        done.wait_send()

    def local_run(x_local, coef_local, targets_local, step_local):
        samples, blk = x_local.shape
        vmem = pl.BlockSpec(memory_space=pltpu.VMEM)
        hbm = pl.BlockSpec(memory_space=pltpu.HBM)
        w_t, r_t = pl.pallas_call(
            body,
            out_shape=(jax.ShapeDtypeStruct((3, blk), jnp.float32), jax.ShapeDtypeStruct((ROWS, samples), jnp.float32)),
            in_specs=[hbm, vmem, hbm, vmem],
            out_specs=(vmem, vmem),
            scratch_shapes=[
                pltpu.VMEM((samples, blk), jnp.bfloat16),
                pltpu.VMEM((8, blk), jnp.float32),
                pltpu.VMEM((8, blk), jnp.bfloat16),
                pltpu.VMEM((group, ROWS, PIECE), jnp.bfloat16),
                pltpu.VMEM((group, ROWS, PIECE), jnp.bfloat16),
                pltpu.VMEM((ROWS, PIECE), jnp.bfloat16),
                pltpu.VMEM((group, ROWS, PIECE), jnp.bfloat16),
                pltpu.VMEM((ROWS, PIECE), jnp.float32),
                pltpu.VMEM((8, blk), jnp.float32),
                pltpu.SemaphoreType.DMA((8,)),
                pltpu.SemaphoreType.DMA,
                pltpu.SemaphoreType.DMA, pltpu.SemaphoreType.DMA,
                pltpu.SemaphoreType.DMA, pltpu.SemaphoreType.DMA,
                pltpu.SemaphoreType.DMA, pltpu.SemaphoreType.DMA,
            ],
            compiler_params=pltpu.CompilerParams(collective_id=0, has_side_effects=True, vmem_limit_bytes=48 * 1024 * 1024),
        )(x_local, coef_local.T, targets_local.T, step_local[None, :])
        return w_t.T, r_t[:3].T

    return jax.shard_map(local_run, mesh=mesh, in_specs=(P('prob', 'feat'), P(('prob', 'feat'), None), P('prob', None), P(('prob', 'feat'))), out_specs=(P(('prob', 'feat'), None), P('prob', None)), check_vma=False)
```

time: 1110 us -> 134 us (0.12)
  waiting for transfers between devices: 1020 us -> 0 us
  Pallas kernels: 0 us -> 129 us
  matrix products: 69.9 us -> 0 us
  between operations: 14.2 us -> 0.65 us
    psum x7 -> x0, waiting for transfers between devices: 1020 us -> none  [summed_product(): return lax.psum(product.astype(jnp.bfloat16).astype(jnp.float32), 'feat')]
    pallas_call x0 -> x1, Pallas kernels: none -> 129 us  [local_run(): pl.pallas_call(body, out_shape=(jax.ShapeDtypeStruct((3, blk), jnp.float3...]
    dot_general x13 -> x0, matrix products: 69.9 us -> none  [the longest x7 41.1 us: summed_product(): jnp.dot(x_local, values.astype(jnp.bfloat16), preferred_element_type=jnp....]
  transfers between devices with their start and end apart: 7 -> 0, of which waited for: 7 -> 0; matrix products, arithmetic and copies ran while one was open for 0% -> 0% of each run, Pallas kernels for 0% -> 0%
where the time goes in v1:
time: 134 us
  Pallas kernels  129 us (96%)
  local copies, waits for them, and re-layouts  3.62 us (3%)
    pallas_call x1, Pallas kernels, local_run(): pl.pallas_call(body, out_shape=(jax.ShapeDtypeStruct((3, blk), jnp.float3...  129 us
    unnamed x7, local copies, waits for them, and re-layouts  2.9 us

profile of v1, /device:TPU:1, one launch (start us, length us, event | category | flops | bytes accessed | tf_op | source)
XLA Modules:
  0.0 133.7 jit_solution(10675421434996722053)
XLA Ops:
  0.6 0.0 copy-start
  0.6 0.9 copy-done
  1.6 0.0 copy-start.1
  1.6 0.7 copy-done.1
  2.3 0.0 copy-start.2
  2.3 0.7 copy-done.2
  2.9 129.4 %shard_map.59 = (f32[3,256]{1,0:T(4,128)S(1)}, f32[4,16384]{1,0:T(4,128)S(1)}) custom-call(bf16[16384,256]{1,0:T(8,128)(2,1)} %x_hbm.1, f32[3,256]{1,0:T(4,128)S(1)} %bitcast.7, f32[3,16384]{1,0:T(4,128)S(1)} %bitcast.6, f32[1,256]{1,0:T(1,128)S(1)} %bitcast.9), custom_call_target="tpu_custom_call" | custom-call | tf_op jit(solution)/shard_map/pallas_call | solution.py:152
  132.4 0.7 slice_bitcast_fusion
  133.1 0.6 copy.7
Async XLA Ops:
  0.6 1.0 copy-start
  1.6 0.7 copy-start.1
  2.3 0.7 copy-start.2
